TPU v7x, 32 devices: a whole 2x2x4 slice. The times are simulated.
32 devices in a mesh: gx: 4 (over z), gy: 4 (over x, core), gz: 2 (over y).
Axes of the slice: x: 2, y: 2, z: 4, core: 2. Of those that a mesh axis runs over, the one named last changes fastest.
Arguments:
- source: float32 [64, 32, 512], P('gx', 'gz', 'gy'), may hold values from -0.6 to 0.6
- shift: float32 [1], replicated, may hold values from 1e-05 to 0.0001
Outputs:
- solution: float32 [64, 32, 512], P('gx', 'gz', 'gy')
All inputs are finite; a program needn't handle non-finite values.
Results may differ from a plain program's by a relative error of at most 0.0004.
Values sent between devices are 32-bit elements; how exact they have to be, the bound alone decides.
No kernel may reach another device: no remote copies, remote signals or barrier semaphores. Data moves between devices by JAX's collectives and lax.ppermute only.
A program may use at most 64 MiB of HBM per device.

v0:
```python
import math

import jax
import jax.numpy as jnp
import numpy as np
from jax import lax
from jax.experimental import pallas as pl
from jax.experimental.pallas import tpu as pltpu
from jax.sharding import PartitionSpec as P

LEVELS = 4


DAMPING = 6.0 / 7.0
PRECISE = lax.Precision.HIGHEST
CUBIC_EVEN = (-5.0 / 128.0, 35.0 / 128.0, 105.0 / 128.0, -7.0 / 128.0)
CUBIC_ODD = (-7.0 / 128.0, 105.0 / 128.0, 35.0 / 128.0, -5.0 / 128.0)
LINEAR_EVEN = (0.25, 0.75)
LINEAR_ODD = (0.75, 0.25)


def extended(block, sides, width):
    for axis, dim in sides:
        count = lax.axis_size(axis)
        forward = [(i, i + 1) for i in range(count - 1)]
        forward.append((count - 1, 0))
        backward = [(target, source) for source, target in forward]
        low = lax.ppermute(
            lax.slice_in_dim(block, block.shape[dim] - width, None, axis=dim), axis, forward
        )
        high = lax.ppermute(lax.slice_in_dim(block, 0, width, axis=dim), axis, backward)
        block = jnp.concatenate([low, block, high], axis=dim)
    return block


def wrapped(values, width):
    return jnp.pad(values, width, mode="wrap")


def neighbours(padded):
    center = padded[1:-1, 1:-1, 1:-1]
    beside_all = padded[2:, 1:-1, 1:-1] + padded[:-2, 1:-1, 1:-1]
    beside_all = beside_all + padded[1:-1, 2:, 1:-1] + padded[1:-1, :-2, 1:-1]
    beside_all = beside_all + padded[1:-1, 1:-1, 2:] + padded[1:-1, 1:-1, :-2]
    return (center, beside_all)


def defect(padded, forcing, weight_nb, diagonal):
    center, beside_all = neighbours(padded)
    return forcing - (diagonal * center - weight_nb * beside_all)


def relaxed(padded, forcing, weight_nb, diagonal):
    center, beside_all = neighbours(padded)
    return center + DAMPING * (forcing - (diagonal * center - weight_nb * beside_all)) / diagonal


def coarsen(values):
    values = values[0::2] + values[1::2]
    values = values[:, 0::2] + values[:, 1::2]
    values = values[:, :, 0::2] + values[:, :, 1::2]
    return 0.125 * values


def refine_axis(padded, dimension, even_weights, odd_weights):
    margin = len(even_weights) // 2
    length = padded.shape[dimension] - 2 * margin
    even_cells = even_weights[0] * lax.slice_in_dim(padded, 0, length, axis=dimension)
    odd_cells = odd_weights[0] * lax.slice_in_dim(padded, 1, 1 + length, axis=dimension)
    for offset in range(1, len(even_weights)):
        even_cells = even_cells + even_weights[offset] * lax.slice_in_dim(
            padded, offset, offset + length, axis=dimension
        )
        odd_cells = odd_cells + odd_weights[offset] * lax.slice_in_dim(
            padded, offset + 1, offset + 1 + length, axis=dimension
        )
    stacked = jnp.stack([even_cells, odd_cells], axis=dimension + 1)
    new_shape = list(even_cells.shape)
    new_shape[dimension] = 2 * length
    return stacked.reshape(new_shape)


def refine(padded, even_weights, odd_weights):
    for dimension in range(3):
        padded = refine_axis(padded, dimension, even_weights, odd_weights)
    return padded


def tables(cells_count):
    indices = jnp.arange(cells_count, dtype=jnp.int32)
    angles = (indices[:, None] * indices[None, :] % cells_count).astype(jnp.float32) * (
        2.0 * math.pi / cells_count
    )
    return (jnp.cos(angles), jnp.sin(angles))


def along_axis(matrix, values, dimension):
    product = jnp.tensordot(matrix, values, axes=([1], [dimension]), precision=PRECISE)
    return jnp.moveaxis(product, 0, dimension)


def coarse_solve(forcing, shift_value, weight_nb):
    cosine_table, sine_table = tables(forcing.shape[0])
    real_part = along_axis(cosine_table, forcing, 0)
    imag_part = -along_axis(sine_table, forcing, 0)
    for dimension in (1, 2):
        cosine_table, sine_table = tables(forcing.shape[dimension])
        real_next = along_axis(cosine_table, real_part, dimension) + along_axis(
            sine_table, imag_part, dimension
        )
        imag_part = along_axis(cosine_table, imag_part, dimension) - along_axis(
            sine_table, real_part, dimension
        )
        real_part = real_next
    cosines = [
        jnp.cos(jnp.arange(cells_count, dtype=jnp.float32) * (2.0 * math.pi / cells_count))
        for cells_count in forcing.shape
    ]
    eigenvalue = (
        weight_nb
        * (
            6.0
            - 2.0 * cosines[0][:, None, None]
            - 2.0 * cosines[1][None, :, None]
            - 2.0 * cosines[2][None, None, :]
        )
        + shift_value
    )
    real_part = real_part / eigenvalue
    imag_part = imag_part / eigenvalue
    for dimension in (0, 1):
        cosine_table, sine_table = tables(forcing.shape[dimension])
        real_next = along_axis(cosine_table, real_part, dimension) - along_axis(
            sine_table, imag_part, dimension
        )
        imag_part = along_axis(cosine_table, imag_part, dimension) + along_axis(
            sine_table, real_part, dimension
        )
        real_part = real_next
    cosine_table, sine_table = tables(forcing.shape[2])
    real_part = along_axis(cosine_table, real_part, 2) - along_axis(sine_table, imag_part, 2)
    return real_part / float(forcing.size)


def vcycle_whole(grid_level, iterate, forcing, shift_value):
    weight_nb = 0.25**grid_level
    diagonal = 6.0 * weight_nb + shift_value
    if iterate is None:
        iterate = DAMPING * forcing / diagonal
    else:
        iterate = relaxed(wrapped(iterate, 1), forcing, weight_nb, diagonal)
    residue = coarsen(defect(wrapped(iterate, 1), forcing, weight_nb, diagonal))
    if grid_level + 1 == LEVELS - 1:
        correction = coarse_solve(residue, shift_value, 0.25 ** (grid_level + 1))
    else:
        correction = vcycle_whole(grid_level + 1, None, residue, shift_value)
    iterate = iterate + refine(wrapped(correction, 1), LINEAR_EVEN, LINEAR_ODD)
    return relaxed(wrapped(iterate, 1), forcing, weight_nb, diagonal)


def collect(block):
    axes = ("gx", "gy", "gz")
    counts = [lax.axis_size(axis) for axis in axes]
    copies = jnp.broadcast_to(block[None], (math.prod(counts),) + block.shape)
    gathered = lax.all_to_all(copies, axes, 0, 0)
    extent_first, extent_second, extent_third = block.shape
    gathered = gathered.reshape(counts + list(block.shape))
    gathered = jnp.transpose(gathered, (0, 3, 2, 4, 1, 5))
    return gathered.reshape(
        counts[0] * extent_first, counts[2] * extent_second, counts[1] * extent_third
    )


def own_block(whole, width, block_shape):
    padded = jnp.pad(whole, width, mode="wrap")
    starts = (
        lax.axis_index("gx") * block_shape[0],
        lax.axis_index("gz") * block_shape[1],
        lax.axis_index("gy") * block_shape[2],
    )
    extents = (block_shape[0] + 2 * width, block_shape[1] + 2 * width, block_shape[2] + 2 * width)
    return lax.dynamic_slice(padded, starts, extents)


def face_halo(block):
    corners = jnp.pad(block, 1)
    for axis, dim in (("gx", 0), ("gy", 2), ("gz", 1)):
        count = lax.axis_size(axis)
        forward = [(i, (i + 1) % count) for i in range(count)]
        backward = [(target, source) for source, target in forward]
        extent = block.shape[dim]
        low = lax.ppermute(
            lax.slice_in_dim(block, extent - 1, None, axis=dim), axis, forward
        )
        high = lax.ppermute(lax.slice_in_dim(block, 0, 1, axis=dim), axis, backward)
        starts = [1, 1, 1]
        starts[dim] = 0
        corners = lax.dynamic_update_slice(corners, low, starts)
        starts[dim] = extent + 1
        corners = lax.dynamic_update_slice(corners, high, starts)
    return corners


def per_device_plain(source, shift):
    shift_value = shift[0]
    source_rim = face_halo(source)
    own_coarse = coarsen(source)
    sources = [None, collect(own_coarse)]
    for grid_level in range(2, LEVELS):
        sources.append(coarsen(sources[-1]))
    whole = coarse_solve(sources[-1], shift_value, 0.25 ** (LEVELS - 1))
    for grid_level in range(LEVELS - 2, 0, -1):
        whole = refine(wrapped(whole, 2), CUBIC_EVEN, CUBIC_ODD)
        whole = vcycle_whole(grid_level, whole, sources[grid_level], shift_value)
    diagonal = 6.0 + shift_value
    iterate = refine(own_block(whole, 3, own_coarse.shape), CUBIC_EVEN, CUBIC_ODD)
    iterate = relaxed(iterate, source_rim, 1.0, diagonal)
    residue = coarsen(defect(iterate, source, 1.0, diagonal))
    correction = vcycle_whole(1, None, collect(residue), shift_value)
    rim = refine(own_block(correction, 2, own_coarse.shape), LINEAR_EVEN, LINEAR_ODD)
    iterate = iterate + rim[1:-1, 1:-1, 1:-1]
    return relaxed(iterate, source, 1.0, diagonal)


def halving(count):
    matrix = np.zeros((count // 2, count))
    for cell in range(count):
        matrix[cell // 2, cell] = 1.0
    return matrix


def doubling(cells, count, even_weights, odd_weights, start=0, periodic=True):
    matrix = np.zeros((len(cells), count))
    margin = len(even_weights) // 2
    for row, cell in enumerate(cells):
        if cell is None:
            continue
        weights = odd_weights if cell % 2 else even_weights
        first = cell // 2 - margin + cell % 2
        for offset, weight in enumerate(weights):
            column = first + offset - start
            matrix[row, column % count if periodic else column] += weight
    return matrix


def pieces(matrix):
    rest = np.asarray(matrix, np.float64)
    found = []
    while np.any(rest) and len(found) < 3:
        part = rest.astype(jnp.bfloat16)
        found.append(part)
        rest = rest - part.astype(np.float64)
    return found


def ring_cells(extent, total, margin):
    cells = [None] * total
    for cell in range(-margin, extent + margin):
        cells[cell % total] = cell
    return cells


def split_values(values):
    high = values.astype(jnp.bfloat16)
    rest = values - high.astype(jnp.float32)
    middle = rest.astype(jnp.bfloat16)
    low = (rest - middle.astype(jnp.float32)).astype(jnp.bfloat16)
    return (low, middle, high)


def from_left(matrix_refs, values):
    total = None
    parts = split_values(values)
    for matrix_ref in reversed(matrix_refs):
        for part in parts:
            term = jnp.dot(matrix_ref[...], part, preferred_element_type=jnp.float32)
            total = term if total is None else total + term
    return total


def from_right(values, matrix_refs):
    total = None
    parts = split_values(values)
    for matrix_ref in reversed(matrix_refs):
        for part in parts:
            term = jnp.dot(part, matrix_ref[...], preferred_element_type=jnp.float32)
            total = term if total is None else total + term
    return total


def flat(values):
    return values.reshape(values.shape[0] * values.shape[1], values.shape[2])


def beside_rolled(values, periodic_first):
    if periodic_first:
        total = jnp.concatenate([values[1:], values[:1]], axis=0) + jnp.concatenate(
            [values[-1:], values[:-1]], axis=0
        )
        center = values
    else:
        total = values[2:] + values[:-2]
        center = values[1:-1]
    for axis in (1, 2):
        extent = values.shape[axis]
        total = total + (pltpu.roll(center, 1, axis) + pltpu.roll(center, extent - 1, axis))
    return (center, total)


def defect_rolled(values, forcing, weight_nb, diagonal, periodic_first=True):
    center, total = beside_rolled(values, periodic_first)
    return forcing - (diagonal * center - weight_nb * total)


def damping_over(diagonal, extent):
    return jnp.full((1, 1, extent), DAMPING, jnp.float32) / diagonal


def sweep_rolled(values, forcing, weight_nb, diagonal, periodic_first=True):
    center, total = beside_rolled(values, periodic_first)
    scale = damping_over(diagonal, values.shape[2])
    return center + scale * (forcing - (diagonal * center - weight_nb * total))


def level_tables(grid_level, shape):
    first, second, third = shape
    found = {}
    found["rows_down"] = pieces(np.kron(halving(first), halving(second)))
    found["lanes_down"] = pieces(0.125 * halving(third).T)
    for name, even, odd in (
        ("linear", LINEAR_EVEN, LINEAR_ODD),
        ("cubic", CUBIC_EVEN, CUBIC_ODD),
    ):
        up = [doubling(range(count), count // 2, even, odd) for count in shape]
        found["rows_" + name] = pieces(np.kron(up[0], up[1]))
        found["lanes_" + name] = pieces(up[2].T)
    return {(grid_level, name): value for name, value in found.items()}


def solve_tables(shape):
    def hartley(count):
        indices = np.arange(count)
        angles = 2.0 * np.pi * (indices[:, None] * indices[None, :] % count) / count
        return np.cos(angles) + np.sin(angles)

    cosines = [np.cos(2.0 * np.pi * np.arange(count) / count) for count in shape]
    spread = (
        6.0
        - 2.0 * cosines[0][:, None, None]
        - 2.0 * cosines[1][None, :, None]
        - 2.0 * cosines[2][None, None, :]
    )
    spread = 0.25 ** (LEVELS - 1) * spread.reshape(shape[0] * shape[1], shape[2])
    rows = np.kron(hartley(shape[0]), hartley(shape[1]))
    return {
        ("solve", "rows"): [rows.astype(np.float32)],
        ("solve", "lanes"): [hartley(shape[2]).astype(np.float32)],
        ("solve", "spread"): [spread.astype(np.float32)],
    }


def solve_rolled(tables_of, forcing, shift_value):
    rows = tables_of["solve", "rows"][0][...]
    lanes = tables_of["solve", "lanes"][0][...]

    def transform(values):
        values = jnp.dot(rows, values, precision=PRECISE, preferred_element_type=jnp.float32)
        return jnp.dot(values, lanes, precision=PRECISE, preferred_element_type=jnp.float32)

    modes = transform(forcing) / (tables_of["solve", "spread"][0][...] + shift_value)
    return transform(modes) * (1.0 / forcing.size)


def down(tables_of, grid_level, values):
    coarse = from_left(tables_of[grid_level, "rows_down"], flat(values))
    return from_right(coarse, tables_of[grid_level, "lanes_down"])


def up(tables_of, grid_level, name, values, shape):
    wide = from_right(values, tables_of[grid_level, "lanes_" + name])
    return from_left(tables_of[grid_level, "rows_" + name], wide).reshape(shape)


def vcycle_rolled(tables_of, grid_level, iterate, forcing, shift_value):
    weight_nb = 0.25**grid_level
    diagonal = 6.0 * weight_nb + shift_value
    shape = forcing.shape
    if iterate is None:
        iterate = damping_over(diagonal, shape[2]) * forcing
    else:
        iterate = sweep_rolled(iterate, forcing, weight_nb, diagonal)
    residue = down(tables_of, grid_level, defect_rolled(iterate, forcing, weight_nb, diagonal))
    if grid_level + 1 == LEVELS - 1:
        correction = solve_rolled(tables_of, residue, shift_value)
    else:
        coarse_shape = tuple(extent // 2 for extent in shape)
        correction = flat(
            vcycle_rolled(
                tables_of, grid_level + 1, None, residue.reshape(coarse_shape), shift_value
            )
        )
    iterate = iterate + up(tables_of, grid_level, "linear", correction, shape)
    return sweep_rolled(iterate, forcing, weight_nb, diagonal)


def pack(tables_of, values):
    coarse = from_left(tables_of["own", "rows_down"], flat(values))
    half = coarse.shape[0] // 2
    return from_right(coarse[:half], tables_of["own", "left_down"]) + from_right(
        coarse[half:], tables_of["own", "right_down"]
    )


def unpack(gathered_ref, whole_ref, counts, extents):
    half, second, lanes = (extents[0] // 2, extents[1], 2 * extents[2])
    low_lane = lax.broadcasted_iota(jnp.int32, (half, second, lanes), 2) < extents[2]
    for x in range(counts[0]):
        for z in range(counts[2]):
            for pair in range(counts[1] // 2):
                blocks = [
                    gathered_ref[(x * counts[1] + 2 * pair + side) * counts[2] + z].reshape(
                        half, second, lanes
                    )
                    for side in range(2)
                ]
                turned = [pltpu.roll(block, extents[2], 2) for block in blocks]
                window = (pl.ds(z * second, second), pl.ds(pair * lanes, lanes))
                whole_ref[(pl.ds(x * 2 * half, half), *window)] = jnp.where(
                    low_lane, blocks[0], turned[1]
                )
                whole_ref[(pl.ds(x * 2 * half + half, half), *window)] = jnp.where(
                    low_lane, turned[0], blocks[1]
                )


def own_window(whole, scratch_ref, margin, extents, place_ref):
    count = whole.shape[0]
    scratch_ref[pl.ds(margin, count)] = whole
    scratch_ref[pl.ds(0, margin)] = whole[count - margin :]
    scratch_ref[pl.ds(margin + count, margin)] = whole[:margin]
    cut = scratch_ref[pl.ds(place_ref[0] * extents[0], extents[0] + 2 * margin)]
    turn_second = (whole.shape[1] - place_ref[1] * extents[1]) % whole.shape[1]
    turn_third = (whole.shape[2] - place_ref[2] * extents[2]) % whole.shape[2]
    return pltpu.roll(pltpu.roll(cut, turn_second, 1), turn_third, 2)


def with_tables(body, tables_map, n_plain):
    keys = [(key, len(value)) for key, value in tables_map.items()]
    arrays = [jnp.asarray(part) for value in tables_map.values() for part in value]

    def kernel(*refs):
        position = n_plain
        tables_of = {}
        for key, length in keys:
            tables_of[key] = refs[position : position + length]
            position += length
        body(tables_of, refs[:n_plain], refs[position:])

    return (kernel, arrays)


def per_device_kernels(source, shift):
    counts = tuple(lax.axis_size(axis) for axis in ("gx", "gy", "gz"))
    block = source.shape
    extents = tuple(extent // 2 for extent in block)
    shape = (extents[0] * counts[0], extents[1] * counts[2], extents[2] * counts[1])
    place = jnp.stack([lax.axis_index("gx"), lax.axis_index("gz"), lax.axis_index("gy")])
    devices = math.prod(counts)
    rows_wide = block[1] + 8
    lanes_wide = 2 * block[2]
    vmem = pl.BlockSpec(memory_space=pltpu.VMEM)
    smem = pl.BlockSpec(memory_space=pltpu.SMEM)

    own = {("own", "rows_down"): pieces(np.kron(halving(block[0]), halving(block[1])))}
    narrow = 0.125 * halving(block[2]).T
    own["own", "left_down"] = pieces(np.concatenate([narrow, 0.0 * narrow], axis=1))
    own["own", "right_down"] = pieces(np.concatenate([0.0 * narrow, narrow], axis=1))

    def edge_tables(name, even, odd, margin):
        fine = margin
        coarse = len(even) // 2 + 1
        first = doubling(
            range(-fine, block[0] + fine), extents[0] + 2 * coarse, even, odd, -coarse, False
        )
        second = doubling(ring_cells(block[1], rows_wide, fine), shape[1], even, odd)
        third = doubling(ring_cells(block[2], lanes_wide, fine), shape[2], even, odd)
        return {
            ("own", "rows_" + name): pieces(np.kron(first, second)),
            ("own", "lanes_" + name): pieces(third.T),
        }

    levels = {}
    for grid_level in range(1, LEVELS - 1):
        levels.update(
            level_tables(grid_level, tuple(extent >> (grid_level - 1) for extent in shape))
        )
    levels.update(solve_tables(tuple(extent >> (LEVELS - 2) for extent in shape)))

    def gather(copies):
        return lax.all_to_all(copies, ("gx", "gy", "gz"), 0, 0)

    copies_shape = jax.ShapeDtypeStruct(
        (devices, extents[0] // 2 * extents[1], 2 * extents[2]), jnp.float32
    )

    def pack_body(tables_of, ins, outs):
        outs[0][...] = jnp.broadcast_to(pack(tables_of, ins[0][...])[None], copies_shape.shape)

    kernel, arrays = with_tables(pack_body, own, 1)
    copies = pl.pallas_call(
        kernel,
        out_shape=copies_shape,
        in_specs=[vmem] * (1 + len(arrays)),
        out_specs=vmem,
        name="pack",
    )(source, *arrays)

    rims = []
    for axis, dim in (("gx", 0), ("gz", 1), ("gy", 2)):
        count = lax.axis_size(axis)
        forward = [(i, (i + 1) % count) for i in range(count)]
        backward = [(target, origin) for origin, target in forward]
        rims.append(
            lax.ppermute(
                lax.slice_in_dim(source, block[dim] - 1, None, axis=dim), axis, forward
            )
        )
        rims.append(lax.ppermute(lax.slice_in_dim(source, 0, 1, axis=dim), axis, backward))
    gathered = gather(copies)

    def first_body(tables_of, ins, outs):
        shift_ref, place_ref, gathered_ref, source_ref = ins[:4]
        low_first, high_first, low_second, high_second, low_third, high_third = ins[4:]
        copies_ref, iterate_ref, whole_ref, scratch_ref = outs
        shift_value = shift_ref[0]
        unpack(gathered_ref, whole_ref, counts, extents)
        whole_forcing = whole_ref[...]
        forcings = [whole_forcing]
        for grid_level in range(1, LEVELS - 1):
            fine = forcings[-1]
            coarse = down(tables_of, grid_level, fine)
            if grid_level + 1 < LEVELS - 1:
                coarse = coarse.reshape(tuple(extent // 2 for extent in fine.shape))
            forcings.append(coarse)
        iterate = solve_rolled(tables_of, forcings[-1], shift_value)
        for grid_level in range(LEVELS - 2, 0, -1):
            forcing = forcings[grid_level - 1]
            if iterate.ndim == 3:
                iterate = flat(iterate)
            iterate = up(tables_of, grid_level, "cubic", iterate, forcing.shape)
            iterate = vcycle_rolled(tables_of, grid_level, iterate, forcing, shift_value)
        window = own_window(iterate, scratch_ref, 3, extents, place_ref)
        iterate = from_right(flat(window), tables_of["own", "lanes_cubic"])
        iterate = from_left(tables_of["own", "rows_cubic"], iterate)
        iterate = iterate.reshape(block[0] + 4, rows_wide, lanes_wide)

        wide = (block[0], rows_wide, lanes_wide)
        row = lax.broadcasted_iota(jnp.int32, wide, 1)
        lane = lax.broadcasted_iota(jnp.int32, wide, 2)

        def widened(values):
            first = values.shape[0]
            values = jnp.concatenate([values, jnp.zeros_like(values[:, :8])], axis=1)
            return jnp.concatenate([values, jnp.zeros((first, rows_wide, block[2]))], axis=2)

        def rows_only(values):
            values = jnp.concatenate([values, jnp.zeros_like(values)], axis=2)
            return jnp.broadcast_to(values, wide)

        def lanes_only(values):
            values = jnp.broadcast_to(values, (block[0], block[1], lanes_wide))
            return jnp.concatenate([values, jnp.zeros_like(values[:, :8])], axis=1)

        middle = widened(source_ref[...])
        middle = jnp.where(row == block[1], rows_only(high_second[...]), middle)
        middle = jnp.where(row == rows_wide - 1, rows_only(low_second[...]), middle)
        middle = jnp.where(lane == block[2], lanes_only(high_third[...]), middle)
        middle = jnp.where(lane == lanes_wide - 1, lanes_only(low_third[...]), middle)
        forcing = jnp.concatenate(
            [widened(low_first[...]), middle, widened(high_first[...])], axis=0
        )
        diagonal = 6.0 + shift_value
        iterate = sweep_rolled(iterate, forcing, 1.0, diagonal, False)
        iterate_ref[...] = iterate
        residue = defect_rolled(iterate, middle, 1.0, diagonal, False)
        packed = pack(tables_of, residue[:, : block[1], : block[2]])
        copies_ref[...] = jnp.broadcast_to(packed[None], copies_ref.shape)

    tables_map = {**levels, **own, **edge_tables("cubic", CUBIC_EVEN, CUBIC_ODD, 2)}
    kernel, arrays = with_tables(first_body, tables_map, 10)
    iterate_shape = jax.ShapeDtypeStruct((block[0] + 2, rows_wide, lanes_wide), jnp.float32)
    copies, iterate = pl.pallas_call(
        kernel,
        out_shape=(copies_shape, iterate_shape),
        in_specs=[smem, smem] + [vmem] * (8 + len(arrays)),
        out_specs=(vmem, vmem),
        scratch_shapes=[
            pltpu.VMEM(shape, jnp.float32),
            pltpu.VMEM((shape[0] + 6, *shape[1:]), jnp.float32),
        ],
        name="first",
    )(shift, place, gathered, source, *rims, *arrays)
    gathered = gather(copies)

    def second_body(tables_of, ins, outs):
        shift_ref, place_ref, gathered_ref, source_ref, iterate_ref = ins
        result_ref, whole_ref, scratch_ref = outs
        shift_value = shift_ref[0]
        unpack(gathered_ref, whole_ref, counts, extents)
        correction = vcycle_rolled(tables_of, 1, None, whole_ref[...], shift_value)
        window = own_window(correction, scratch_ref, 2, extents, place_ref)
        wide = from_right(flat(window), tables_of["own", "lanes_linear"])
        wide = from_left(tables_of["own", "rows_linear"], wide).reshape(iterate_shape.shape)
        iterate = iterate_ref[...] + wide
        center, total = beside_rolled(iterate, False)
        center = center[:, : block[1], : block[2]]
        total = total[:, : block[1], : block[2]]
        diagonal = 6.0 + shift_value
        scale = damping_over(diagonal, block[2])
        result_ref[...] = center + scale * (source_ref[...] - (diagonal * center - total))

    tables_map = {key: value for key, value in levels.items() if "cubic" not in key[1]}
    tables_map.update(edge_tables("linear", LINEAR_EVEN, LINEAR_ODD, 1))
    kernel, arrays = with_tables(second_body, tables_map, 5)
    return pl.pallas_call(
        kernel,
        out_shape=jax.ShapeDtypeStruct(block, jnp.float32),
        in_specs=[smem, smem] + [vmem] * (3 + len(arrays)),
        out_specs=vmem,
        scratch_shapes=[
            pltpu.VMEM(shape, jnp.float32),
            pltpu.VMEM((shape[0] + 4, *shape[1:]), jnp.float32),
        ],
        name="second",
    )(shift, place, gathered, source, iterate, *arrays)


WHOLE_LIMIT = 1 << 18


def per_device(source, shift):
    block = source.shape
    counts = tuple(lax.axis_size(axis) for axis in ("gx", "gy", "gz"))
    cells = math.prod(block) // 8 * math.prod(counts)
    second_deep = block[1] * counts[2] >> (LEVELS - 2)
    third_deep = block[2] * counts[1] >> (LEVELS - 2)
    aligned = (
        block[0] % 4 == 0
        and block[1] % 16 == 0
        and block[2] == 128
        and counts[1] % 2 == 0
        and second_deep % 8 == 0
        and third_deep % 128 == 0
        and block[0] * counts[0] >= 32
    )
    if aligned and cells <= WHOLE_LIMIT:
        return per_device_kernels(source, shift)
    return per_device_plain(source, shift)


def solution(mesh):
    in_specs = (P("gx", "gz", "gy"), P())
    out_specs = P("gx", "gz", "gy")
    return jax.shard_map(
        per_device, mesh=mesh, in_specs=in_specs, out_specs=out_specs, check_vma=False
    )
```

profile of v0, /device:TPU:1, one launch (start us, length us, event | category | flops | bytes accessed | tf_op | source)
XLA Modules:
  0.0 63.9 jit_solution(14285152510589973445)
XLA Ops:
  0.0 2.2 %pack.1 = f32[32,32,128]{2,1,0:T(8,128)} custom-call(f32[16,16,128]{2,1,0:T(8,128)} %refs_3_.4, bf16[64,256]{1,0:T(8,128)(2,1)} %constant.61.clone.refs_1_.refs_27_, bf16[128,128]{1,0:T(8,128)(2,1)} %constant.62.clone.refs_2_.refs_28_, bf16[128,128]{1,0:T(8,128)(2,1)} %constant.63.clone.refs_3_.refs_29_), custom_call_target="tpu_custom_call" | custom-call | tf_op jit(solution)/shard_map/pack/pallas_call | solution.py:510
  2.2 0.0 copy-start
  2.2 7.1 %all-to-all-start = ((f32[32,32,128]{2,1,0:T(8,128)}), f32[32,32,128]{2,1,0:T(8,128)S(1)}, u32[]{:S(2)}, u32[]{:S(2)}) async-start(f32[32,32,128]{2,1,0:T(8,128)} %pack.1), calls=%async_computation | async-start | bytes 1048576 | tf_op jit(solution)/shard_map/all_to_all | solution.py:500
  9.2 0.0 copy-done
  9.3 1.4 %collective-permute-start.3 = (f32[16,1,128]{2,1,0:T(1,128)S(1)}, f32[16,1,128]{2,1,0:T(1,128)S(1)}, u32[]{:S(2)}, u32[]{:S(2)}) collective-permute-start(f32[16,1,128]{2,1,0:T(1,128)S(1)} %get-tuple-element.11), channel_id=1, source_target_pairs={{1,0},{0,1},{3,2},{2,3},{5,4},{4,5},{7,6},{6,7},{9,8},{8,9},{11,10... | collective-permute-start | bytes 24584 | tf_op jit(solution)/shard_map/ppermute | solution.py:528
  10.7 0.1 collective-permute-start.2
  10.8 0.1 fusion
  10.9 0.9 %collective-permute-start.5 = (f32[16,16,1]{2,1,0:T(8,128)S(1)}, f32[16,16,1]{2,1,0:T(8,128)S(1)}, u32[]{:S(2)}, u32[]{:S(2)}) collective-permute-start(f32[16,16,1]{2,1,0:T(8,128)S(1)} %get-tuple-element.9), channel_id=1, source_target_pairs={{2,0},{4,2},{6,4},{0,6},{3,1},{5,3},{7,5},{1,7},{10,8},{12,10},{14... | collective-permute-start | bytes 3080 | tf_op jit(solution)/shard_map/ppermute | solution.py:528
  11.8 3.3 %collective-permute-start.1 = (f32[1,16,128]{2,1,0:T(8,128)S(1)}, f32[1,16,128]{2,1,0:T(8,128)S(1)}, u32[]{:S(2)}, u32[]{:S(2)}) collective-permute-start(f32[1,16,128]{2,1,0:T(8,128)S(1)} %get-tuple-element.13), channel_id=1, source_target_pairs={{8,0},{16,8},{24,16},{0,24},{9,1},{17,9},{25,17},{1,25},{10,2},{18... | collective-permute-start | bytes 24584 | tf_op jit(solution)/shard_map/ppermute | solution.py:528
  15.1 0.0 collective-permute-start
  15.1 2.4 %collective-permute-done.5.refs_9_ = f32[16,16,1]{2,1,0:T(8,128)S(1)} collective-permute-done((f32[16,16,1]{2,1,0:T(8,128)S(1)}, f32[16,16,1]{2,1,0:T(8,128)S(1)}, u32[]{:S(2)}, u32[]{:S(2)}) %collective-permute-start.5) | collective-permute-done | bytes 1056 | tf_op jit(solution)/shard_map/ppermute | solution.py:528
  17.6 0.0 collective-permute-start.4
  17.6 0.7 %pad_add_fusion.refs_1_ = s32[3]{0:T(128)} fusion(s32[1]{0:T(128)} %bitcast.2, s32[1]{0:T(128)} %bitcast.1, s32[1]{0:T(128)} %bitcast), kind=kLoop, calls=%fused_computation | loop fusion | flops 6 | bytes 24 | tf_op jit(solution)/shard_map/stack | solution.py:467
  18.9 1.0 %collective-permute-done.4.refs_8_ = f32[16,16,1]{2,1,0:T(8,128)S(1)} collective-permute-done((f32[16,16,1]{2,1,0:T(8,128)S(1)}, f32[16,16,1]{2,1,0:T(8,128)S(1)}, u32[]{:S(2)}, u32[]{:S(2)}) %collective-permute-start.4) | collective-permute-done | bytes 1056 | tf_op jit(solution)/shard_map/ppermute | solution.py:524
  19.8 0.0 collective-permute-done.3.refs_7_
  19.8 0.0 collective-permute-done.2.refs_6_
  19.8 0.0 copy-start.5
  19.8 0.0 collective-permute-done.1.refs_5_
  19.9 0.0 copy-start.6
  19.9 2.1 %collective-permute-done.refs_4_ = f32[1,16,128]{2,1,0:T(8,128)S(1)} collective-permute-done((f32[1,16,128]{2,1,0:T(8,128)S(1)}, f32[1,16,128]{2,1,0:T(8,128)S(1)}, u32[]{:S(2)}, u32[]{:S(2)}) %collective-permute-start) | collective-permute-done | bytes 8224 | tf_op jit(solution)/shard_map/ppermute | solution.py:524
  22.0 3.3 %all-to-all-done.refs_2_ = f32[32,32,128]{2,1,0:T(8,128)S(1)} async-done(((f32[32,32,128]{2,1,0:T(8,128)}), f32[32,32,128]{2,1,0:T(8,128)S(1)}, u32[]{:S(2)}, u32[]{:S(2)}) %all-to-all-start) | async-done | bytes 524320 | tf_op jit(solution)/shard_map/all_to_all | solution.py:500
  25.3 0.0 copy-done.2
  25.3 0.0 copy-done.3
  25.3 0.0 copy-done.4
  25.3 0.0 copy-done.5
  25.3 0.0 copy-done.6
  25.3 0.0 copy-done.7
  25.4 0.0 copy-start.1
  25.4 0.8 %copy-done.1 = f32[32,32,128]{2,1,0:T(8,128)} copy-done((f32[32,32,128]{2,1,0:T(8,128)}, f32[32,32,128]{2,1,0:T(8,128)S(1)}, u32[]{:S(2)}) %copy-start.1) | copy-done | bytes 524312
  26.2 12.5 %first.1 = (f32[32,32,128]{2,1,0:T(8,128)}, f32[18,24,256]{2,1,0:T(8,128)}) custom-call(f32[1]{0:T(128)S(6)} %copy.28.refs_0_, s32[3]{0:T(128)} %pad_add_fusion.refs_1_, f32[32,32,128]{2,1,0:T(8,128)} %copy-done.1, f32[16,16,128]{2,1,0:T(8,128)} %refs_3_.4, f32[1,16,128]{2,1,0:T(8,128)} %copy-done.7, f32[1,16,128]{2,1,0:T(8,128)} %copy-done.6, ...), custom_call_target="tpu_custom_call" | custom-call | tf_op jit(solution)/shard_map/first/pallas_call | solution.py:592
  38.7 18.8 %all_to_all.10.refs_2_ = f32[32,32,128]{2,1,0:T(8,128)} all-to-all(f32[32,32,128]{2,1,0:T(8,128)} %get-tuple-element.7), channel_id=1, replica_groups=mesh['gx'=4,'gy'=4,'gz'=2] {'gx','gy','gz'}, dimensions={0} | all-to-all | bytes 1048576 | tf_op jit(solution)/shard_map/all_to_all | solution.py:500
  57.4 6.5 %second.1 = f32[16,16,128]{2,1,0:T(8,128)} custom-call(f32[1]{0:T(128)S(6)} %copy.28.refs_0_, s32[3]{0:T(128)} %pad_add_fusion.refs_1_, f32[32,32,128]{2,1,0:T(8,128)} %all_to_all.10.refs_2_, f32[16,16,128]{2,1,0:T(8,128)} %refs_3_.4, f32[18,24,256]{2,1,0:T(8,128)} %get-tuple-element.8.refs_4_, bf16[128,512]{1,0:T(8,128)(2,1)} %constant.64.clone.refs_10_.refs_5_, ...), custom_call_target="tpu_custom_call" | custom-call | tf_op jit(solution)/shard_map/second/pallas_call | solution.py:625
  (6 shorter events, 0.0 us)
Async XLA Ops:
  2.2 7.1 %copy-start = (f32[16,16,128]{2,1,0:T(8,128)S(1)}, f32[16,16,128]{2,1,0:T(8,128)}, u32[]{:S(2)}) copy-start(f32[16,16,128]{2,1,0:T(8,128)} %refs_3_.4) | copy-start | bytes 393220
  2.2 23.2 %all-to-all-start = ((f32[32,32,128]{2,1,0:T(8,128)}), f32[32,32,128]{2,1,0:T(8,128)S(1)}, u32[]{:S(2)}, u32[]{:S(2)}) async-start(f32[32,32,128]{2,1,0:T(8,128)} %pack.1), calls=%async_computation | async-start | bytes 1048576 | tf_op jit(solution)/shard_map/all_to_all | solution.py:500
  9.3 10.5 %collective-permute-start.3 = (f32[16,1,128]{2,1,0:T(1,128)S(1)}, f32[16,1,128]{2,1,0:T(1,128)S(1)}, u32[]{:S(2)}, u32[]{:S(2)}) collective-permute-start(f32[16,1,128]{2,1,0:T(1,128)S(1)} %get-tuple-element.11), channel_id=1, source_target_pairs={{1,0},{0,1},{3,2},{2,3},{5,4},{4,5},{7,6},{6,7},{9,8},{8,9},{11,10... | collective-permute-start | bytes 24584 | tf_op jit(solution)/shard_map/ppermute | solution.py:528
  10.7 9.1 %collective-permute-start.2 = (f32[16,1,128]{2,1,0:T(1,128)S(1)}, f32[16,1,128]{2,1,0:T(1,128)S(1)}, u32[]{:S(2)}, u32[]{:S(2)}) collective-permute-start(f32[16,1,128]{2,1,0:T(1,128)S(1)} %get-tuple-element.12), channel_id=1, source_target_pairs={{0,1},{1,0},{2,3},{3,2},{4,5},{5,4},{6,7},{7,6},{8,9},{9,8},{10,11... | collective-permute-start | bytes 24584 | tf_op jit(solution)/shard_map/ppermute | solution.py:524
  10.9 6.6 %collective-permute-start.5 = (f32[16,16,1]{2,1,0:T(8,128)S(1)}, f32[16,16,1]{2,1,0:T(8,128)S(1)}, u32[]{:S(2)}, u32[]{:S(2)}) collective-permute-start(f32[16,16,1]{2,1,0:T(8,128)S(1)} %get-tuple-element.9), channel_id=1, source_target_pairs={{2,0},{4,2},{6,4},{0,6},{3,1},{5,3},{7,5},{1,7},{10,8},{12,10},{14... | collective-permute-start | bytes 3080 | tf_op jit(solution)/shard_map/ppermute | solution.py:528
  11.8 8.1 %collective-permute-start.1 = (f32[1,16,128]{2,1,0:T(8,128)S(1)}, f32[1,16,128]{2,1,0:T(8,128)S(1)}, u32[]{:S(2)}, u32[]{:S(2)}) collective-permute-start(f32[1,16,128]{2,1,0:T(8,128)S(1)} %get-tuple-element.13), channel_id=1, source_target_pairs={{8,0},{16,8},{24,16},{0,24},{9,1},{17,9},{25,17},{1,25},{10,2},{18... | collective-permute-start | bytes 24584 | tf_op jit(solution)/shard_map/ppermute | solution.py:528
  15.1 6.9 %collective-permute-start = (f32[1,16,128]{2,1,0:T(8,128)S(1)}, f32[1,16,128]{2,1,0:T(8,128)S(1)}, u32[]{:S(2)}, u32[]{:S(2)}) collective-permute-start(f32[1,16,128]{2,1,0:T(8,128)S(1)} %get-tuple-element.14), channel_id=1, source_target_pairs={{0,8},{8,16},{16,24},{24,0},{1,9},{9,17},{17,25},{25,1},{2,10},{10... | collective-permute-start | bytes 24584 | tf_op jit(solution)/shard_map/ppermute | solution.py:524
  17.6 7.8 %copy-start.2 = (f32[16,16,1]{2,1,0:T(8,128)}, f32[16,16,1]{2,1,0:T(8,128)S(1)}, u32[]{:S(2)}) copy-start(f32[16,16,1]{2,1,0:T(8,128)S(1)} %collective-permute-done.5.refs_9_) | copy-start | bytes 3076
  17.6 2.3 %collective-permute-start.4 = (f32[16,16,1]{2,1,0:T(8,128)S(1)}, f32[16,16,1]{2,1,0:T(8,128)S(1)}, u32[]{:S(2)}, u32[]{:S(2)}) collective-permute-start(f32[16,16,1]{2,1,0:T(8,128)S(1)} %get-tuple-element.10), channel_id=1, source_target_pairs={{0,2},{2,4},{4,6},{6,0},{1,3},{3,5},{5,7},{7,1},{8,10},{10,12},{12... | collective-permute-start | bytes 3080 | tf_op jit(solution)/shard_map/ppermute | solution.py:524
  19.8 5.5 %copy-start.3 = (f32[16,16,1]{2,1,0:T(8,128)}, f32[16,16,1]{2,1,0:T(8,128)S(1)}, u32[]{:S(2)}) copy-start(f32[16,16,1]{2,1,0:T(8,128)S(1)} %collective-permute-done.4.refs_8_) | copy-start | bytes 3076
  19.8 5.5 %copy-start.4 = (f32[16,1,128]{2,1,0:T(1,128)}, f32[16,1,128]{2,1,0:T(1,128)S(1)}, u32[]{:S(2)}) copy-start(f32[16,1,128]{2,1,0:T(1,128)S(1)} %collective-permute-done.3.refs_7_) | copy-start | bytes 24580
  19.8 5.5 %copy-start.5 = (f32[16,1,128]{2,1,0:T(1,128)}, f32[16,1,128]{2,1,0:T(1,128)S(1)}, u32[]{:S(2)}) copy-start(f32[16,1,128]{2,1,0:T(1,128)S(1)} %collective-permute-done.2.refs_6_) | copy-start | bytes 24580
  19.9 5.5 %copy-start.6 = (f32[1,16,128]{2,1,0:T(8,128)}, f32[1,16,128]{2,1,0:T(8,128)S(1)}, u32[]{:S(2)}) copy-start(f32[1,16,128]{2,1,0:T(8,128)S(1)} %collective-permute-done.1.refs_5_) | copy-start | bytes 24580
  22.0 3.3 %copy-start.7 = (f32[1,16,128]{2,1,0:T(8,128)}, f32[1,16,128]{2,1,0:T(8,128)S(1)}, u32[]{:S(2)}) copy-start(f32[1,16,128]{2,1,0:T(8,128)S(1)} %collective-permute-done.refs_4_) | copy-start | bytes 24580
  25.4 0.8 %copy-start.1 = (f32[32,32,128]{2,1,0:T(8,128)}, f32[32,32,128]{2,1,0:T(8,128)S(1)}, u32[]{:S(2)}) copy-start(f32[32,32,128]{2,1,0:T(8,128)S(1)} %all-to-all-done.refs_2_) | copy-start | bytes 1572868
where the time goes:
time: 64.3 us; the launch traced here: 63.9 us
  Pallas kernels  21.2 us (33%)
  blocking collectives  18.8 us (29%)
  starting transfers between devices  12.8 us (20%)
  waiting for transfers between devices  8.83 us (14%)
  local copies, waits for them, and re-layouts  0.92 us (1%)
  between operations  0.76 us (1%)
  other arithmetic  0.65 us (1%)
    all_to_all x1, blocking collectives, gather(): return lax.all_to_all(copies, ('gx', 'gy', 'gz'), 0, 0)  18.8 us
    pallas_call x1, Pallas kernels, per_device_kernels(): pl.pallas_call(kernel, out_shape=(copies_shape, iterate_shape), in_specs=...  12.5 us
    all_to_all x1, starting transfers between devices, gather(): return lax.all_to_all(copies, ('gx', 'gy', 'gz'), 0, 0)  7.08 us
    pallas_call x1, Pallas kernels, per_device_kernels(): pl.pallas_call(kernel, out_shape=jax.ShapeDtypeStruct(block, jnp.float32)...  6.49 us
    ppermute x3, starting transfers between devices, per_device_kernels(): lax.ppermute(lax.slice_in_dim(source, 0, 1, axis=dim), axis, backward)  5.63 us
    all_to_all x1, waiting for transfers between devices, gather(): return lax.all_to_all(copies, ('gx', 'gy', 'gz'), 0, 0)  3.3 us
    ppermute x3, waiting for transfers between devices, per_device_kernels(): lax.ppermute(lax.slice_in_dim(source, block[dim] - 1, None, axis=dim), ax...  3.1 us
    ppermute x3, waiting for transfers between devices, per_device_kernels(): lax.ppermute(lax.slice_in_dim(source, 0, 1, axis=dim), axis, backward)  2.43 us
  transfers between devices with their start and end apart: 7, of which 4 were waited for; matrix products, arithmetic and copies ran while one was open for 1% of the time, Pallas kernels for 0%

commit v1 on v0

--- a/solution.py
+++ b/solution.py
@@ -271,9 +271,9 @@
 def from_left(matrix_refs, values):
     total = None
     parts = split_values(values)
-    for matrix_ref in reversed(matrix_refs):
-        for part in parts:
-            term = jnp.dot(matrix_ref[...], part, preferred_element_type=jnp.float32)
+    for piece in reversed(range(len(matrix_refs))):
+        for part in parts[piece:]:
+            term = jnp.dot(matrix_refs[piece][...], part, preferred_element_type=jnp.float32)
             total = term if total is None else total + term
     return total
 
@@ -281,9 +281,9 @@
 def from_right(values, matrix_refs):
     total = None
     parts = split_values(values)
-    for matrix_ref in reversed(matrix_refs):
-        for part in parts:
-            term = jnp.dot(part, matrix_ref[...], preferred_element_type=jnp.float32)
+    for piece in reversed(range(len(matrix_refs))):
+        for part in parts[piece:]:
+            term = jnp.dot(part, matrix_refs[piece][...], preferred_element_type=jnp.float32)
             total = term if total is None else total + term
     return total
 
@@ -337,7 +337,46 @@
     return {(grid_level, name): value for name, value in found.items()}
 
 
-def solve_tables(shape):
+def kept_products(length):
+    return [(piece, part) for piece in range(length) for part in range(3 - piece)]
+
+
+def joined(matrix, axis):
+    found = pieces(matrix)
+    order = [found[piece] for piece, _ in kept_products(len(found))]
+    return [np.concatenate(order, axis=axis)]
+
+
+def join_values(values, length, axis):
+    parts = split_values(values)[::-1]
+    chosen = [parts[part] for _, part in kept_products(length)]
+    return jnp.concatenate(chosen, axis=axis)
+
+
+def pieces_joined(joined_extent, extent):
+    for length in (1, 2, 3):
+        if len(kept_products(length)) * extent == joined_extent:
+            return length
+    raise ValueError("table extent")
+
+
+def joined_left(table_ref, values):
+    length = pieces_joined(table_ref.shape[1], values.shape[0])
+    return jnp.dot(
+        table_ref[...], join_values(values, length, 0), preferred_element_type=jnp.float32
+    )
+
+
+def joined_right(values, table_ref):
+    length = pieces_joined(table_ref.shape[0], values.shape[1])
+    return jnp.dot(
+        join_values(values, length, 1), table_ref[...], preferred_element_type=jnp.float32
+    )
+
+
+def solve_tables(fine_shape):
+    shape = tuple(count // 2 for count in fine_shape)
+
     def hartley(count):
         indices = np.arange(count)
         angles = 2.0 * np.pi * (indices[:, None] * indices[None, :] % count) / count
@@ -351,24 +390,34 @@
         - 2.0 * cosines[2][None, None, :]
     )
     spread = 0.25 ** (LEVELS - 1) * spread.reshape(shape[0] * shape[1], shape[2])
-    rows = np.kron(hartley(shape[0]), hartley(shape[1]))
-    return {
-        ("solve", "rows"): [rows.astype(np.float32)],
-        ("solve", "lanes"): [hartley(shape[2]).astype(np.float32)],
+    padding = -shape[2] % 128
+    spread = np.pad(spread, ((0, 0), (0, padding)), constant_values=1.0)
+    to_modes = [hartley(coarse) @ halving(fine) for coarse, fine in zip(shape, fine_shape)]
+    found = {
+        ("solve", "rows_to"): joined(np.kron(to_modes[0], to_modes[1]), 1),
+        ("solve", "lanes_to"): joined(np.pad(0.125 * to_modes[2].T, ((0, 0), (0, padding))), 0),
         ("solve", "spread"): [spread.astype(np.float32)],
     }
-
-
-def solve_rolled(tables_of, forcing, shift_value):
-    rows = tables_of["solve", "rows"][0][...]
-    lanes = tables_of["solve", "lanes"][0][...]
-
-    def transform(values):
-        values = jnp.dot(rows, values, precision=PRECISE, preferred_element_type=jnp.float32)
-        return jnp.dot(values, lanes, precision=PRECISE, preferred_element_type=jnp.float32)
-
-    modes = transform(forcing) / (tables_of["solve", "spread"][0][...] + shift_value)
-    return transform(modes) * (1.0 / forcing.size)
+    for name, even, odd in (
+        ("linear", LINEAR_EVEN, LINEAR_ODD),
+        ("cubic", CUBIC_EVEN, CUBIC_ODD),
+    ):
+        back = [
+            doubling(range(fine), coarse, even, odd) @ hartley(coarse) / coarse
+            for coarse, fine in zip(shape, fine_shape)
+        ]
+        found["solve", "rows_" + name] = joined(np.kron(back[0], back[1]), 1)
+        found["solve", "lanes_" + name] = joined(np.pad(back[2].T, ((0, padding), (0, 0))), 0)
+    return found
+
+
+def solve_up(tables_of, name, forcing, shift_value):
+    modes = joined_left(tables_of["solve", "rows_to"][0], flat(forcing))
+    modes = joined_right(modes, tables_of["solve", "lanes_to"][0])
+    modes = modes / (tables_of["solve", "spread"][0][...] + shift_value)
+    wide = joined_right(modes, tables_of["solve", "lanes_" + name][0])
+    wide = joined_left(tables_of["solve", "rows_" + name][0], wide)
+    return wide.reshape(forcing.shape)
 
 
 def down(tables_of, grid_level, values):
@@ -389,17 +438,18 @@
         iterate = damping_over(diagonal, shape[2]) * forcing
     else:
         iterate = sweep_rolled(iterate, forcing, weight_nb, diagonal)
-    residue = down(tables_of, grid_level, defect_rolled(iterate, forcing, weight_nb, diagonal))
+    residue = defect_rolled(iterate, forcing, weight_nb, diagonal)
     if grid_level + 1 == LEVELS - 1:
-        correction = solve_rolled(tables_of, residue, shift_value)
+        iterate = iterate + solve_up(tables_of, "linear", residue, shift_value)
     else:
+        residue = down(tables_of, grid_level, residue)
         coarse_shape = tuple(extent // 2 for extent in shape)
         correction = flat(
             vcycle_rolled(
                 tables_of, grid_level + 1, None, residue.reshape(coarse_shape), shift_value
             )
         )
-    iterate = iterate + up(tables_of, grid_level, "linear", correction, shape)
+        iterate = iterate + up(tables_of, grid_level, "linear", correction, shape)
     return sweep_rolled(iterate, forcing, weight_nb, diagonal)
 
 
@@ -490,11 +540,11 @@
         }
 
     levels = {}
-    for grid_level in range(1, LEVELS - 1):
+    for grid_level in range(1, LEVELS - 2):
         levels.update(
             level_tables(grid_level, tuple(extent >> (grid_level - 1) for extent in shape))
         )
-    levels.update(solve_tables(tuple(extent >> (LEVELS - 2) for extent in shape)))
+    levels.update(solve_tables(tuple(extent >> (LEVELS - 3) for extent in shape)))
 
     def gather(copies):
         return lax.all_to_all(copies, ("gx", "gy", "gz"), 0, 0)
@@ -504,50 +554,65 @@
     )
 
     def pack_body(tables_of, ins, outs):
-        outs[0][...] = jnp.broadcast_to(pack(tables_of, ins[0][...])[None], copies_shape.shape)
+        values = ins[0][...]
+        outs[0][...] = jnp.broadcast_to(pack(tables_of, values)[None], copies_shape.shape)
+        lane = lax.broadcasted_iota(jnp.int32, block, 2)
+        square = (block[0], block[1], block[1])
+        same = lax.broadcasted_iota(jnp.int32, square, 1) == lax.broadcasted_iota(
+            jnp.int32, square, 2
+        )
+        for out_ref, chosen in ((outs[1], block[2] - 1), (outs[2], 0)):
+            face = jnp.sum(jnp.where(lane == chosen, values, 0.0), axis=2, keepdims=True)
+            face = jnp.where(same, jnp.broadcast_to(face, square), 0.0)
+            out_ref[...] = jnp.sum(face, axis=1, keepdims=True)
 
     kernel, arrays = with_tables(pack_body, own, 1)
-    copies = pl.pallas_call(
+    face_shape = jax.ShapeDtypeStruct((block[0], 1, block[1]), jnp.float32)
+    copies, last_third, first_third = pl.pallas_call(
         kernel,
-        out_shape=copies_shape,
+        out_shape=(copies_shape, face_shape, face_shape),
         in_specs=[vmem] * (1 + len(arrays)),
-        out_specs=vmem,
+        out_specs=(vmem, vmem, vmem),
         name="pack",
     )(source, *arrays)
 
-    rims = []
-    for axis, dim in (("gx", 0), ("gz", 1), ("gy", 2)):
+    def ring_shift(values, axis, step):
         count = lax.axis_size(axis)
-        forward = [(i, (i + 1) % count) for i in range(count)]
-        backward = [(target, origin) for origin, target in forward]
+        return lax.ppermute(values, axis, [(i, (i + step) % count) for i in range(count)])
+
+    rims = [
+        ring_shift(source[block[0] - 1 :], "gx", 1),
+        ring_shift(source[:1], "gx", -1),
+    ]
+    last_second = source[:, block[1] - 1 :]
+    first_second = source[:, :1]
+    if counts[2] == 2:
+        rims.append(ring_shift(jnp.stack([last_second, first_second]), "gz", 1))
+    else:
         rims.append(
-            lax.ppermute(
-                lax.slice_in_dim(source, block[dim] - 1, None, axis=dim), axis, forward
-            )
-        )
-        rims.append(lax.ppermute(lax.slice_in_dim(source, 0, 1, axis=dim), axis, backward))
+            jnp.stack([ring_shift(last_second, "gz", 1), ring_shift(first_second, "gz", -1)])
+        )
+    rims.append(ring_shift(last_third, "gy", 1))
+    rims.append(ring_shift(first_third, "gy", -1))
     gathered = gather(copies)
 
     def first_body(tables_of, ins, outs):
         shift_ref, place_ref, gathered_ref, source_ref = ins[:4]
-        low_first, high_first, low_second, high_second, low_third, high_third = ins[4:]
+        low_first, high_first, both_second, low_third, high_third = ins[4:]
         copies_ref, iterate_ref, whole_ref, scratch_ref = outs
         shift_value = shift_ref[0]
         unpack(gathered_ref, whole_ref, counts, extents)
         whole_forcing = whole_ref[...]
         forcings = [whole_forcing]
-        for grid_level in range(1, LEVELS - 1):
+        for grid_level in range(1, LEVELS - 2):
             fine = forcings[-1]
             coarse = down(tables_of, grid_level, fine)
-            if grid_level + 1 < LEVELS - 1:
-                coarse = coarse.reshape(tuple(extent // 2 for extent in fine.shape))
-            forcings.append(coarse)
-        iterate = solve_rolled(tables_of, forcings[-1], shift_value)
+            forcings.append(coarse.reshape(tuple(extent // 2 for extent in fine.shape)))
+        iterate = solve_up(tables_of, "cubic", forcings[-1], shift_value)
         for grid_level in range(LEVELS - 2, 0, -1):
             forcing = forcings[grid_level - 1]
-            if iterate.ndim == 3:
-                iterate = flat(iterate)
-            iterate = up(tables_of, grid_level, "cubic", iterate, forcing.shape)
+            if grid_level < LEVELS - 2:
+                iterate = up(tables_of, grid_level, "cubic", flat(iterate), forcing.shape)
             iterate = vcycle_rolled(tables_of, grid_level, iterate, forcing, shift_value)
         window = own_window(iterate, scratch_ref, 3, extents, place_ref)
         iterate = from_right(flat(window), tables_of["own", "lanes_cubic"])
@@ -568,12 +633,18 @@
             return jnp.broadcast_to(values, wide)
 
         def lanes_only(values):
+            square = (block[0], block[1], block[1])
+            same = lax.broadcasted_iota(jnp.int32, square, 1) == lax.broadcasted_iota(
+                jnp.int32, square, 2
+            )
+            values = jnp.where(same, jnp.broadcast_to(values, square), 0.0)
+            values = jnp.sum(values, axis=2, keepdims=True)
             values = jnp.broadcast_to(values, (block[0], block[1], lanes_wide))
             return jnp.concatenate([values, jnp.zeros_like(values[:, :8])], axis=1)
 
         middle = widened(source_ref[...])
-        middle = jnp.where(row == block[1], rows_only(high_second[...]), middle)
-        middle = jnp.where(row == rows_wide - 1, rows_only(low_second[...]), middle)
+        middle = jnp.where(row == block[1], rows_only(both_second[1]), middle)
+        middle = jnp.where(row == rows_wide - 1, rows_only(both_second[0]), middle)
         middle = jnp.where(lane == block[2], lanes_only(high_third[...]), middle)
         middle = jnp.where(lane == lanes_wide - 1, lanes_only(low_third[...]), middle)
         forcing = jnp.concatenate(
@@ -587,12 +658,12 @@
         copies_ref[...] = jnp.broadcast_to(packed[None], copies_ref.shape)
 
     tables_map = {**levels, **own, **edge_tables("cubic", CUBIC_EVEN, CUBIC_ODD, 2)}
-    kernel, arrays = with_tables(first_body, tables_map, 10)
+    kernel, arrays = with_tables(first_body, tables_map, 9)
     iterate_shape = jax.ShapeDtypeStruct((block[0] + 2, rows_wide, lanes_wide), jnp.float32)
     copies, iterate = pl.pallas_call(
         kernel,
         out_shape=(copies_shape, iterate_shape),
-        in_specs=[smem, smem] + [vmem] * (8 + len(arrays)),
+        in_specs=[smem, smem] + [vmem] * (7 + len(arrays)),
         out_specs=(vmem, vmem),
         scratch_shapes=[
             pltpu.VMEM(shape, jnp.float32),

time: 64.3 us -> 61.8 us (0.961)
  Pallas kernels: 21.2 us -> 18.5 us
  waiting for transfers between devices: 8.83 us -> 6.53 us
  local copies, waits for them, and re-layouts: 0.92 us -> 2.43 us
  starting transfers between devices: 12.8 us -> 13.6 us
    ppermute x6 -> x5, waiting for transfers between devices: 5.53 us -> 3.23 us  [ring_shift(): lax.ppermute(values, axis, [(i, (i + step) % count) for i in range(count)])]
    pallas_call x1, Pallas kernels: 12.5 us -> 10.4 us  [per_device_kernels(): pl.pallas_call(kernel, out_shape=(copies_shape, iterate_shape), in_specs=...]
    another operation x0 -> x1, local copies, waits for them, and re-layouts: none -> 0.88 us  [per_device_kernels(): rims.append(ring_shift(jnp.stack([last_second, first_second]), 'gz', 1))]
    ppermute x6 -> x5, starting transfers between devices: 5.75 us -> 6.53 us  [ring_shift(): lax.ppermute(values, axis, [(i, (i + step) % count) for i in range(count)])]
  transfers between devices with their start and end apart: 7 -> 6, of which waited for: 4 -> 3; matrix products, arithmetic and copies ran while one was open for 1% -> 4% of each run, Pallas kernels for 0% -> 0%
where the time goes in v1:
time: 61.8 us; the launch traced here: 61.3 us
  blocking collectives  18.8 us (30%)
  Pallas kernels  18.5 us (30%)
  starting transfers between devices  13.6 us (22%)
  waiting for transfers between devices  6.53 us (11%)
  local copies, waits for them, and re-layouts  2.43 us (4%)
  between operations  0.75 us (1%)
  other arithmetic  0.68 us (1%)
    all_to_all x1, blocking collectives, gather(): return lax.all_to_all(copies, ('gx', 'gy', 'gz'), 0, 0)  18.8 us
    pallas_call x1, Pallas kernels, per_device_kernels(): pl.pallas_call(kernel, out_shape=(copies_shape, iterate_shape), in_specs=...  10.4 us
    all_to_all x1, starting transfers between devices, gather(): return lax.all_to_all(copies, ('gx', 'gy', 'gz'), 0, 0)  7.08 us
    ppermute x5, starting transfers between devices, ring_shift(): lax.ppermute(values, axis, [(i, (i + step) % count) for i in range(count)])  6.53 us
    pallas_call x1, Pallas kernels, per_device_kernels(): pl.pallas_call(kernel, out_shape=jax.ShapeDtypeStruct(block, jnp.float32)...  5.97 us
    all_to_all x1, waiting for transfers between devices, gather(): return lax.all_to_all(copies, ('gx', 'gy', 'gz'), 0, 0)  3.3 us
    ppermute x5, waiting for transfers between devices, ring_shift(): lax.ppermute(values, axis, [(i, (i + step) % count) for i in range(count)])  3.23 us
    pallas_call x1, Pallas kernels, per_device_kernels(): pl.pallas_call(kernel, out_shape=(copies_shape, face_shape, face_shape),...  2.17 us
  transfers between devices with their start and end apart: 6, of which 3 were waited for; matrix products, arithmetic and copies ran while one was open for 4% of the time, Pallas kernels for 0%

profile of v1, /device:TPU:1, one launch (start us, length us, event | category | flops | bytes accessed | tf_op | source)
XLA Modules:
  0.0 61.3 jit_solution(8999327005176552909)
XLA Ops:
  0.0 2.2 %pack.1 = (f32[32,32,128]{2,1,0:T(8,128)}, f32[16,1,16]{2,1,0:T(1,128)}, f32[16,1,16]{2,1,0:T(1,128)}) custom-call(f32[16,16,128]{2,1,0:T(8,128)} %refs_3_.4, bf16[64,256]{1,0:T(8,128)(2,1)} %constant.55.clone.refs_1_.refs_23_, bf16[128,128]{1,0:T(8,128)(2,1)} %constant.56.clone.refs_2_.refs_24_, bf16[128,128]{1,0:T(8,128)(2,1)} %constant.57.clone.refs_3_.refs_25_), custom_call_target="tpu_custom_call" | custom-call | tf_op jit(solution)/shard_map/pack/pallas_call | solution.py:571
  2.2 7.1 %all-to-all-start = ((f32[32,32,128]{2,1,0:T(8,128)}), f32[32,32,128]{2,1,0:T(8,128)S(1)}, u32[]{:S(2)}, u32[]{:S(2)}) async-start(f32[32,32,128]{2,1,0:T(8,128)} %get-tuple-element.10), calls=%async_computation | async-start | bytes 1048576 | tf_op jit(solution)/shard_map/all_to_all | solution.py:550
  9.3 0.7 %fusion = (f32[1,16,128]{2,1,0:T(8,128)S(1)}, f32[1,16,128]{2,1,0:T(8,128)S(1)}) fusion(f32[16,16,128]{2,1,0:T(8,128)} %refs_3_.4), kind=kLoop, calls=%fused_computation.4 | loop fusion | bytes 32768 | tf_op jit(solution)/shard_map/slice | solution.py:585
  10.0 3.2 %collective-permute-start.1 = (f32[1,16,128]{2,1,0:T(8,128)S(1)}, f32[1,16,128]{2,1,0:T(8,128)S(1)}, u32[]{:S(2)}, u32[]{:S(2)}) collective-permute-start(f32[1,16,128]{2,1,0:T(8,128)S(1)} %get-tuple-element.17), channel_id=1, source_target_pairs={{0,24},{8,0},{16,8},{24,16},{1,25},{9,1},{17,9},{25,17},{2,26},{10... | collective-permute-start | bytes 24584 | tf_op jit(solution)/shard_map/ppermute | solution.py:581
  13.2 0.0 collective-permute-start
  13.2 0.9 %slice_bitcast_fusion.1 = (f32[1,16,1,128]{3,2,1,0:T(1,128)S(1)}, f32[1,16,1,128]{3,2,1,0:T(1,128)S(1)}) fusion(f32[16,16,128]{2,1,0:T(8,128)} %refs_3_.4), kind=kLoop, calls=%fused_computation.2 | loop fusion | bytes 32768 | tf_op jit(solution)/shard_map/stack | solution.py:590
  14.1 0.0 copy-start.7
  14.1 0.0 copy-start.6
  14.1 1.3 %collective-permute-start.2 = (f32[2,16,1,128]{3,2,1,0:T(1,128)S(1)}, f32[2,16,1,128]{3,2,1,0:T(1,128)S(1)}, u32[]{:S(2)}, u32[]{:S(2)}) collective-permute-start(f32[2,16,1,128]{3,2,1,0:T(1,128)S(1)} %pad_maximum_fusion), channel_id=1, source_target_pairs={{0,1},{1,0},{2,3},{3,2},{4,5},{5,4},{6,7},{7,6},{8,9},{9,8},{10,11... | collective-permute-start | bytes 49160 | tf_op jit(solution)/shard_map/ppermute | solution.py:581
  15.4 0.0 copy-done.7
  15.4 2.0 %collective-permute-start.3 = (f32[16,1,16]{2,1,0:T(1,128)S(1)}, f32[16,1,16]{2,1,0:T(1,128)S(1)}, u32[]{:S(2)}, u32[]{:S(2)}) collective-permute-start(f32[16,1,16]{2,1,0:T(1,128)S(1)} %copy-done.7), channel_id=1, source_target_pairs={{0,2},{2,4},{4,6},{6,0},{1,3},{3,5},{5,7},{7,1},{8,10},{10,12},{12... | collective-permute-start | bytes 3080 | tf_op jit(solution)/shard_map/ppermute | solution.py:581
  17.4 0.0 copy-done.6
  17.4 0.0 collective-permute-start.4
  17.4 0.7 %pad_add_fusion.refs_1_ = s32[3]{0:T(128)} fusion(s32[1]{0:T(128)} %bitcast.2, s32[1]{0:T(128)} %bitcast.1, s32[1]{0:T(128)} %bitcast), kind=kLoop, calls=%fused_computation.3 | loop fusion | flops 6 | bytes 24 | tf_op jit(solution)/shard_map/stack | solution.py:517
  18.8 0.0 collective-permute-done.3.refs_7_
  18.8 0.0 copy-start.4
  18.8 2.1 %collective-permute-done.4.refs_8_ = f32[16,1,16]{2,1,0:T(1,128)S(1)} collective-permute-done((f32[16,1,16]{2,1,0:T(1,128)S(1)}, f32[16,1,16]{2,1,0:T(1,128)S(1)}, u32[]{:S(2)}, u32[]{:S(2)}) %collective-permute-start.4) | collective-permute-done | bytes 1056 | tf_op jit(solution)/shard_map/ppermute | solution.py:581
  20.8 0.0 copy-start.5
  20.8 0.0 collective-permute-done.1.refs_5_
  20.9 1.2 %collective-permute-done.refs_4_ = f32[1,16,128]{2,1,0:T(8,128)S(1)} collective-permute-done((f32[1,16,128]{2,1,0:T(8,128)S(1)}, f32[1,16,128]{2,1,0:T(8,128)S(1)}, u32[]{:S(2)}, u32[]{:S(2)}) %collective-permute-start) | collective-permute-done | bytes 8224 | tf_op jit(solution)/shard_map/ppermute | solution.py:581
  22.0 0.0 collective-permute-done.2.refs_6_
  22.0 3.3 %all-to-all-done.refs_2_ = f32[32,32,128]{2,1,0:T(8,128)S(1)} async-done(((f32[32,32,128]{2,1,0:T(8,128)}), f32[32,32,128]{2,1,0:T(8,128)S(1)}, u32[]{:S(2)}, u32[]{:S(2)}) %all-to-all-start) | async-done | bytes 524320 | tf_op jit(solution)/shard_map/all_to_all | solution.py:550
  25.3 0.0 copy-done.4
  25.3 0.0 copy-done.5
  25.3 0.0 copy-done.2
  25.3 0.0 copy-done.3
  25.3 0.0 copy-done.1
  25.4 0.0 copy-start
  25.4 0.8 %copy-done = f32[32,32,128]{2,1,0:T(8,128)} copy-done((f32[32,32,128]{2,1,0:T(8,128)}, f32[32,32,128]{2,1,0:T(8,128)S(1)}, u32[]{:S(2)}) %copy-start) | copy-done | bytes 524312
  26.2 10.4 %first.1 = (f32[32,32,128]{2,1,0:T(8,128)}, f32[18,24,256]{2,1,0:T(8,128)}) custom-call(f32[1]{0:T(128)S(6)} %copy.29.refs_0_, s32[3]{0:T(128)} %pad_add_fusion.refs_1_, f32[32,32,128]{2,1,0:T(8,128)} %copy-done, f32[16,16,128]{2,1,0:T(8,128)} %refs_3_.4, f32[1,16,128]{2,1,0:T(8,128)} %copy-done.3, f32[1,16,128]{2,1,0:T(8,128)} %copy-done.2, ...), custom_call_target="tpu_custom_call" | custom-call | tf_op jit(solution)/shard_map/first/pallas_call | solution.py:663
  36.6 18.8 %all_to_all.10.refs_2_ = f32[32,32,128]{2,1,0:T(8,128)} all-to-all(f32[32,32,128]{2,1,0:T(8,128)} %get-tuple-element.13), channel_id=1, replica_groups=mesh['gx'=4,'gy'=4,'gz'=2] {'gx','gy','gz'}, dimensions={0} | all-to-all | bytes 1048576 | tf_op jit(solution)/shard_map/all_to_all | solution.py:550
  55.3 6.0 %second.1 = f32[16,16,128]{2,1,0:T(8,128)} custom-call(f32[1]{0:T(128)S(6)} %copy.29.refs_0_, s32[3]{0:T(128)} %pad_add_fusion.refs_1_, f32[32,32,128]{2,1,0:T(8,128)} %all_to_all.10.refs_2_, f32[16,16,128]{2,1,0:T(8,128)} %refs_3_.4, f32[18,24,256]{2,1,0:T(8,128)} %get-tuple-element.14.refs_4_, bf16[128,512]{1,0:T(8,128)(2,1)} %constant.58.clone.refs_9_.refs_5_, ...), custom_call_target="tpu_custom_call" | custom-call | tf_op jit(solution)/shard_map/second/pallas_call | solution.py:696
  (4 shorter events, 0.0 us)
Async XLA Ops:
  2.2 23.2 %all-to-all-start = ((f32[32,32,128]{2,1,0:T(8,128)}), f32[32,32,128]{2,1,0:T(8,128)S(1)}, u32[]{:S(2)}, u32[]{:S(2)}) async-start(f32[32,32,128]{2,1,0:T(8,128)} %get-tuple-element.10), calls=%async_computation | async-start | bytes 1048576 | tf_op jit(solution)/shard_map/all_to_all | solution.py:550
  10.0 10.9 %collective-permute-start.1 = (f32[1,16,128]{2,1,0:T(8,128)S(1)}, f32[1,16,128]{2,1,0:T(8,128)S(1)}, u32[]{:S(2)}, u32[]{:S(2)}) collective-permute-start(f32[1,16,128]{2,1,0:T(8,128)S(1)} %get-tuple-element.17), channel_id=1, source_target_pairs={{0,24},{8,0},{16,8},{24,16},{1,25},{9,1},{17,9},{25,17},{2,26},{10... | collective-permute-start | bytes 24584 | tf_op jit(solution)/shard_map/ppermute | solution.py:581
  13.2 8.8 %collective-permute-start = (f32[1,16,128]{2,1,0:T(8,128)S(1)}, f32[1,16,128]{2,1,0:T(8,128)S(1)}, u32[]{:S(2)}, u32[]{:S(2)}) collective-permute-start(f32[1,16,128]{2,1,0:T(8,128)S(1)} %get-tuple-element.18), channel_id=1, source_target_pairs={{0,8},{8,16},{16,24},{24,0},{1,9},{9,17},{17,25},{25,1},{2,10},{10... | collective-permute-start | bytes 24584 | tf_op jit(solution)/shard_map/ppermute | solution.py:581
  14.1 1.3 %copy-start.7 = (f32[16,1,16]{2,1,0:T(1,128)S(1)}, f32[16,1,16]{2,1,0:T(1,128)}, u32[]{:S(2)}) copy-start(f32[16,1,16]{2,1,0:T(1,128)} %get-tuple-element.11) | copy-start | bytes 3076
  14.1 3.4 %copy-start.6 = (f32[16,1,16]{2,1,0:T(1,128)S(1)}, f32[16,1,16]{2,1,0:T(1,128)}, u32[]{:S(2)}) copy-start(f32[16,1,16]{2,1,0:T(1,128)} %get-tuple-element.12) | copy-start | bytes 3076
  14.1 7.9 %collective-permute-start.2 = (f32[2,16,1,128]{3,2,1,0:T(1,128)S(1)}, f32[2,16,1,128]{3,2,1,0:T(1,128)S(1)}, u32[]{:S(2)}, u32[]{:S(2)}) collective-permute-start(f32[2,16,1,128]{3,2,1,0:T(1,128)S(1)} %pad_maximum_fusion), channel_id=1, source_target_pairs={{0,1},{1,0},{2,3},{3,2},{4,5},{5,4},{6,7},{7,6},{8,9},{9,8},{10,11... | collective-permute-start | bytes 49160 | tf_op jit(solution)/shard_map/ppermute | solution.py:581
  15.4 3.4 %collective-permute-start.3 = (f32[16,1,16]{2,1,0:T(1,128)S(1)}, f32[16,1,16]{2,1,0:T(1,128)S(1)}, u32[]{:S(2)}, u32[]{:S(2)}) collective-permute-start(f32[16,1,16]{2,1,0:T(1,128)S(1)} %copy-done.7), channel_id=1, source_target_pairs={{0,2},{2,4},{4,6},{6,0},{1,3},{3,5},{5,7},{7,1},{8,10},{10,12},{12... | collective-permute-start | bytes 3080 | tf_op jit(solution)/shard_map/ppermute | solution.py:581
  17.4 3.4 %collective-permute-start.4 = (f32[16,1,16]{2,1,0:T(1,128)S(1)}, f32[16,1,16]{2,1,0:T(1,128)S(1)}, u32[]{:S(2)}, u32[]{:S(2)}) collective-permute-start(f32[16,1,16]{2,1,0:T(1,128)S(1)} %copy-done.6), channel_id=1, source_target_pairs={{0,6},{2,0},{4,2},{6,4},{1,7},{3,1},{5,3},{7,5},{8,14},{10,8},{12,... | collective-permute-start | bytes 3080 | tf_op jit(solution)/shard_map/ppermute | solution.py:581
  18.8 6.5 %copy-start.4 = (f32[16,1,16]{2,1,0:T(1,128)}, f32[16,1,16]{2,1,0:T(1,128)S(1)}, u32[]{:S(2)}) copy-start(f32[16,1,16]{2,1,0:T(1,128)S(1)} %collective-permute-done.3.refs_7_) | copy-start | bytes 3076
  20.8 4.5 %copy-start.5 = (f32[16,1,16]{2,1,0:T(1,128)}, f32[16,1,16]{2,1,0:T(1,128)S(1)}, u32[]{:S(2)}) copy-start(f32[16,1,16]{2,1,0:T(1,128)S(1)} %collective-permute-done.4.refs_8_) | copy-start | bytes 3076
  20.9 4.5 %copy-start.2 = (f32[1,16,128]{2,1,0:T(8,128)}, f32[1,16,128]{2,1,0:T(8,128)S(1)}, u32[]{:S(2)}) copy-start(f32[1,16,128]{2,1,0:T(8,128)S(1)} %collective-permute-done.1.refs_5_) | copy-start | bytes 24580
  22.0 3.3 %copy-start.3 = (f32[1,16,128]{2,1,0:T(8,128)}, f32[1,16,128]{2,1,0:T(8,128)S(1)}, u32[]{:S(2)}) copy-start(f32[1,16,128]{2,1,0:T(8,128)S(1)} %collective-permute-done.refs_4_) | copy-start | bytes 24580
  22.0 3.3 %copy-start.1 = (f32[2,16,1,128]{3,2,1,0:T(1,128)}, f32[2,16,1,128]{3,2,1,0:T(1,128)S(1)}, u32[]{:S(2)}) copy-start(f32[2,16,1,128]{3,2,1,0:T(1,128)S(1)} %collective-permute-done.2.refs_6_) | copy-start | bytes 49156
  25.4 0.8 %copy-start = (f32[32,32,128]{2,1,0:T(8,128)}, f32[32,32,128]{2,1,0:T(8,128)S(1)}, u32[]{:S(2)}) copy-start(f32[32,32,128]{2,1,0:T(8,128)S(1)} %all-to-all-done.refs_2_) | copy-start | bytes 1572868

commit v2 on v1

--- a/solution.py
+++ b/solution.py
@@ -546,16 +546,17 @@
         )
     levels.update(solve_tables(tuple(extent >> (LEVELS - 3) for extent in shape)))
 
-    def gather(copies):
+    packed_shape = jax.ShapeDtypeStruct(
+        (extents[0] // 2 * extents[1], 2 * extents[2]), jnp.float32
+    )
+
+    def gather(packed):
+        copies = jnp.broadcast_to(packed[None], (devices,) + packed.shape)
         return lax.all_to_all(copies, ("gx", "gy", "gz"), 0, 0)
-
-    copies_shape = jax.ShapeDtypeStruct(
-        (devices, extents[0] // 2 * extents[1], 2 * extents[2]), jnp.float32
-    )
 
     def pack_body(tables_of, ins, outs):
         values = ins[0][...]
-        outs[0][...] = jnp.broadcast_to(pack(tables_of, values)[None], copies_shape.shape)
+        outs[0][...] = pack(tables_of, values)
         lane = lax.broadcasted_iota(jnp.int32, block, 2)
         square = (block[0], block[1], block[1])
         same = lax.broadcasted_iota(jnp.int32, square, 1) == lax.broadcasted_iota(
@@ -568,9 +569,9 @@
 
     kernel, arrays = with_tables(pack_body, own, 1)
     face_shape = jax.ShapeDtypeStruct((block[0], 1, block[1]), jnp.float32)
-    copies, last_third, first_third = pl.pallas_call(
+    packed, last_third, first_third = pl.pallas_call(
         kernel,
-        out_shape=(copies_shape, face_shape, face_shape),
+        out_shape=(packed_shape, face_shape, face_shape),
         in_specs=[vmem] * (1 + len(arrays)),
         out_specs=(vmem, vmem, vmem),
         name="pack",
@@ -594,12 +595,12 @@
         )
     rims.append(ring_shift(last_third, "gy", 1))
     rims.append(ring_shift(first_third, "gy", -1))
-    gathered = gather(copies)
+    gathered = gather(packed)
 
     def first_body(tables_of, ins, outs):
         shift_ref, place_ref, gathered_ref, source_ref = ins[:4]
         low_first, high_first, both_second, low_third, high_third = ins[4:]
-        copies_ref, iterate_ref, whole_ref, scratch_ref = outs
+        packed_ref, iterate_ref, whole_ref, scratch_ref = outs
         shift_value = shift_ref[0]
         unpack(gathered_ref, whole_ref, counts, extents)
         whole_forcing = whole_ref[...]
@@ -654,15 +655,14 @@
         iterate = sweep_rolled(iterate, forcing, 1.0, diagonal, False)
         iterate_ref[...] = iterate
         residue = defect_rolled(iterate, middle, 1.0, diagonal, False)
-        packed = pack(tables_of, residue[:, : block[1], : block[2]])
-        copies_ref[...] = jnp.broadcast_to(packed[None], copies_ref.shape)
+        packed_ref[...] = pack(tables_of, residue[:, : block[1], : block[2]])
 
     tables_map = {**levels, **own, **edge_tables("cubic", CUBIC_EVEN, CUBIC_ODD, 2)}
     kernel, arrays = with_tables(first_body, tables_map, 9)
     iterate_shape = jax.ShapeDtypeStruct((block[0] + 2, rows_wide, lanes_wide), jnp.float32)
-    copies, iterate = pl.pallas_call(
+    packed, iterate = pl.pallas_call(
         kernel,
-        out_shape=(copies_shape, iterate_shape),
+        out_shape=(packed_shape, iterate_shape),
         in_specs=[smem, smem] + [vmem] * (7 + len(arrays)),
         out_specs=(vmem, vmem),
         scratch_shapes=[
@@ -671,7 +671,7 @@
         ],
         name="first",
     )(shift, place, gathered, source, *rims, *arrays)
-    gathered = gather(copies)
+    gathered = gather(packed)
 
     def second_body(tables_of, ins, outs):
         shift_ref, place_ref, gathered_ref, source_ref, iterate_ref = ins

time: 61.8 us -> 63.6 us (1.029)
  local copies, waits for them, and re-layouts: 2.43 us -> 4.78 us
    broadcast_in_dim x0 -> x2, local copies, waits for them, and re-layouts: none -> 2.35 us  [gather(): copies = jnp.broadcast_to(packed[None], (devices,) + packed.shape)]
where the time goes in v2:
time: 63.6 us; the launch traced here: 62.9 us
  blocking collectives  18.5 us (29%)
  Pallas kernels  18 us (28%)
  starting transfers between devices  13.6 us (21%)
  waiting for transfers between devices  6.6 us (10%)
  local copies, waits for them, and re-layouts  4.78 us (8%)
  between operations  0.75 us (1%)
    all_to_all x1, blocking collectives, gather(): return lax.all_to_all(copies, ('gx', 'gy', 'gz'), 0, 0)  18.5 us
    pallas_call x1, Pallas kernels, per_device_kernels(): pl.pallas_call(kernel, out_shape=(packed_shape, iterate_shape), in_specs=...  10.1 us
    all_to_all x1, starting transfers between devices, gather(): return lax.all_to_all(copies, ('gx', 'gy', 'gz'), 0, 0)  7.08 us
    ppermute x5, starting transfers between devices, ring_shift(): lax.ppermute(values, axis, [(i, (i + step) % count) for i in range(count)])  6.53 us
    pallas_call x1, Pallas kernels, per_device_kernels(): pl.pallas_call(kernel, out_shape=jax.ShapeDtypeStruct(block, jnp.float32)...  5.97 us
    ppermute x5, waiting for transfers between devices, ring_shift(): lax.ppermute(values, axis, [(i, (i + step) % count) for i in range(count)])  3.3 us
    all_to_all x1, waiting for transfers between devices, gather(): return lax.all_to_all(copies, ('gx', 'gy', 'gz'), 0, 0)  3.3 us
    broadcast_in_dim x2, local copies, waits for them, and re-layouts, gather(): copies = jnp.broadcast_to(packed[None], (devices,) + packed.shape)  2.35 us
  transfers between devices with their start and end apart: 6, of which 3 were waited for; matrix products, arithmetic and copies ran while one was open for 4% of the time, Pallas kernels for 0%

profile of v2, /device:TPU:1, one launch (start us, length us, event | category | flops | bytes accessed | tf_op | source)
XLA Modules:
  0.0 62.9 jit_solution(10215837132404781110)
XLA Ops:
  0.0 1.9 %pack.1 = (f32[32,128]{1,0:T(8,128)}, f32[16,1,16]{2,1,0:T(1,128)}, f32[16,1,16]{2,1,0:T(1,128)}) custom-call(f32[16,16,128]{2,1,0:T(8,128)} %refs_3_.4, bf16[64,256]{1,0:T(8,128)(2,1)} %constant.55.clone.refs_1_.refs_23_, bf16[128,128]{1,0:T(8,128)(2,1)} %constant.56.clone.refs_2_.refs_24_, bf16[128,128]{1,0:T(8,128)(2,1)} %constant.57.clone.refs_3_.refs_25_), custom_call_target="tpu_custom_call" | custom-call | tf_op jit(solution)/shard_map/pack/pallas_call | solution.py:572
  1.9 1.6 %broadcast_in_dim.4 = f32[32,32,128]{2,1,0:T(8,128)} broadcast(f32[32,128]{1,0:T(8,128)} %get-tuple-element.10), dimensions={1,2} | broadcast | bytes 540672 | tf_op jit(solution)/shard_map/broadcast_in_dim | solution.py:554
  3.5 7.1 %all-to-all-start = ((f32[32,32,128]{2,1,0:T(8,128)}), f32[32,32,128]{2,1,0:T(8,128)S(1)}, u32[]{:S(2)}, u32[]{:S(2)}) async-start(f32[32,32,128]{2,1,0:T(8,128)} %broadcast_in_dim.4), calls=%async_computation | async-start | bytes 1048576 | tf_op jit(solution)/shard_map/all_to_all | solution.py:555
  10.6 0.7 %fusion = (f32[1,16,128]{2,1,0:T(8,128)S(1)}, f32[1,16,128]{2,1,0:T(8,128)S(1)}) fusion(f32[16,16,128]{2,1,0:T(8,128)} %refs_3_.4), kind=kLoop, calls=%fused_computation.4 | loop fusion | bytes 32768 | tf_op jit(solution)/shard_map/slice | solution.py:586
  11.3 3.2 %collective-permute-start.1 = (f32[1,16,128]{2,1,0:T(8,128)S(1)}, f32[1,16,128]{2,1,0:T(8,128)S(1)}, u32[]{:S(2)}, u32[]{:S(2)}) collective-permute-start(f32[1,16,128]{2,1,0:T(8,128)S(1)} %get-tuple-element.17), channel_id=1, source_target_pairs={{0,24},{8,0},{16,8},{24,16},{1,25},{9,1},{17,9},{25,17},{2,26},{10... | collective-permute-start | bytes 24584 | tf_op jit(solution)/shard_map/ppermute | solution.py:582
  14.5 0.0 collective-permute-start
  14.5 0.9 %slice_bitcast_fusion.1 = (f32[1,16,1,128]{3,2,1,0:T(1,128)S(1)}, f32[1,16,1,128]{3,2,1,0:T(1,128)S(1)}) fusion(f32[16,16,128]{2,1,0:T(8,128)} %refs_3_.4), kind=kLoop, calls=%fused_computation.2 | loop fusion | bytes 32768 | tf_op jit(solution)/shard_map/stack | solution.py:591
  15.4 0.0 copy-start.7
  15.4 0.0 copy-start.6
  15.4 1.3 %collective-permute-start.2 = (f32[2,16,1,128]{3,2,1,0:T(1,128)S(1)}, f32[2,16,1,128]{3,2,1,0:T(1,128)S(1)}, u32[]{:S(2)}, u32[]{:S(2)}) collective-permute-start(f32[2,16,1,128]{3,2,1,0:T(1,128)S(1)} %pad_maximum_fusion), channel_id=1, source_target_pairs={{0,1},{1,0},{2,3},{3,2},{4,5},{5,4},{6,7},{7,6},{8,9},{9,8},{10,11... | collective-permute-start | bytes 49160 | tf_op jit(solution)/shard_map/ppermute | solution.py:582
  16.7 0.0 copy-done.7
  16.7 2.0 %collective-permute-start.3 = (f32[16,1,16]{2,1,0:T(1,128)S(1)}, f32[16,1,16]{2,1,0:T(1,128)S(1)}, u32[]{:S(2)}, u32[]{:S(2)}) collective-permute-start(f32[16,1,16]{2,1,0:T(1,128)S(1)} %copy-done.7), channel_id=1, source_target_pairs={{0,2},{2,4},{4,6},{6,0},{1,3},{3,5},{5,7},{7,1},{8,10},{10,12},{12... | collective-permute-start | bytes 3080 | tf_op jit(solution)/shard_map/ppermute | solution.py:582
  18.8 0.0 copy-done.6
  18.8 0.0 collective-permute-start.4
  18.8 0.6 pad_add_fusion.refs_1_
  20.0 0.0 collective-permute-done.3.refs_7_
  20.0 0.0 copy-start.4
  20.0 2.1 %collective-permute-done.4.refs_8_ = f32[16,1,16]{2,1,0:T(1,128)S(1)} collective-permute-done((f32[16,1,16]{2,1,0:T(1,128)S(1)}, f32[16,1,16]{2,1,0:T(1,128)S(1)}, u32[]{:S(2)}, u32[]{:S(2)}) %collective-permute-start.4) | collective-permute-done | bytes 1056 | tf_op jit(solution)/shard_map/ppermute | solution.py:582
  22.2 0.0 collective-permute-done.1.refs_5_
  22.2 1.2 %collective-permute-done.refs_4_ = f32[1,16,128]{2,1,0:T(8,128)S(1)} collective-permute-done((f32[1,16,128]{2,1,0:T(8,128)S(1)}, f32[1,16,128]{2,1,0:T(8,128)S(1)}, u32[]{:S(2)}, u32[]{:S(2)}) %collective-permute-start) | collective-permute-done | bytes 8224 | tf_op jit(solution)/shard_map/ppermute | solution.py:582
  23.3 0.0 collective-permute-done.2.refs_6_
  23.3 3.3 %all-to-all-done.refs_2_ = f32[32,32,128]{2,1,0:T(8,128)S(1)} async-done(((f32[32,32,128]{2,1,0:T(8,128)}), f32[32,32,128]{2,1,0:T(8,128)S(1)}, u32[]{:S(2)}, u32[]{:S(2)}) %all-to-all-start) | async-done | bytes 524320 | tf_op jit(solution)/shard_map/all_to_all | solution.py:555
  26.6 0.0 copy-done.4
  26.6 0.0 copy-done.5
  26.6 0.0 copy-done.2
  26.7 0.0 copy-done.3
  26.7 0.0 copy-done.1
  26.7 0.8 %copy-done = f32[32,32,128]{2,1,0:T(8,128)} copy-done((f32[32,32,128]{2,1,0:T(8,128)}, f32[32,32,128]{2,1,0:T(8,128)S(1)}, u32[]{:S(2)}) %copy-start) | copy-done | bytes 524312
  27.5 10.1 %first.1 = (f32[32,128]{1,0:T(8,128)}, f32[18,24,256]{2,1,0:T(8,128)}) custom-call(f32[1]{0:T(128)S(6)} %copy.29.refs_0_, s32[3]{0:T(128)} %pad_add_fusion.refs_1_, f32[32,32,128]{2,1,0:T(8,128)} %copy-done, f32[16,16,128]{2,1,0:T(8,128)} %refs_3_.4, f32[1,16,128]{2,1,0:T(8,128)} %copy-done.3, f32[1,16,128]{2,1,0:T(8,128)} %copy-done.2, ...), custom_call_target="tpu_custom_call" | custom-call | tf_op jit(solution)/shard_map/first/pallas_call | solution.py:663
  37.6 0.8 %broadcast_in_dim.5 = f32[32,32,128]{2,1,0:T(8,128)S(1)} broadcast(f32[32,128]{1,0:T(8,128)} %get-tuple-element.13), dimensions={1,2} | broadcast | bytes 540672 | tf_op jit(solution)/shard_map/broadcast_in_dim | solution.py:554
  38.4 18.5 %all_to_all.10.refs_2_ = f32[32,32,128]{2,1,0:T(8,128)} all-to-all(f32[32,32,128]{2,1,0:T(8,128)S(1)} %broadcast_in_dim.5), channel_id=1, replica_groups=mesh['gx'=4,'gy'=4,'gz'=2] {'gx','gy','gz'}, dimensions={0} | all-to-all | bytes 1048576 | tf_op jit(solution)/shard_map/all_to_all | solution.py:555
  57.0 6.0 %second.1 = f32[16,16,128]{2,1,0:T(8,128)} custom-call(f32[1]{0:T(128)S(6)} %copy.29.refs_0_, s32[3]{0:T(128)} %pad_add_fusion.refs_1_, f32[32,32,128]{2,1,0:T(8,128)} %all_to_all.10.refs_2_, f32[16,16,128]{2,1,0:T(8,128)} %refs_3_.4, f32[18,24,256]{2,1,0:T(8,128)} %get-tuple-element.14.refs_4_, bf16[128,512]{1,0:T(8,128)(2,1)} %constant.58.clone.refs_9_.refs_5_, ...), custom_call_target="tpu_custom_call" | custom-call | tf_op jit(solution)/shard_map/second/pallas_call | solution.py:696
  (6 shorter events, 0.0 us)
Async XLA Ops:
  3.5 23.2 %all-to-all-start = ((f32[32,32,128]{2,1,0:T(8,128)}), f32[32,32,128]{2,1,0:T(8,128)S(1)}, u32[]{:S(2)}, u32[]{:S(2)}) async-start(f32[32,32,128]{2,1,0:T(8,128)} %broadcast_in_dim.4), calls=%async_computation | async-start | bytes 1048576 | tf_op jit(solution)/shard_map/all_to_all | solution.py:555
  11.3 10.9 %collective-permute-start.1 = (f32[1,16,128]{2,1,0:T(8,128)S(1)}, f32[1,16,128]{2,1,0:T(8,128)S(1)}, u32[]{:S(2)}, u32[]{:S(2)}) collective-permute-start(f32[1,16,128]{2,1,0:T(8,128)S(1)} %get-tuple-element.17), channel_id=1, source_target_pairs={{0,24},{8,0},{16,8},{24,16},{1,25},{9,1},{17,9},{25,17},{2,26},{10... | collective-permute-start | bytes 24584 | tf_op jit(solution)/shard_map/ppermute | solution.py:582
  14.5 8.8 %collective-permute-start = (f32[1,16,128]{2,1,0:T(8,128)S(1)}, f32[1,16,128]{2,1,0:T(8,128)S(1)}, u32[]{:S(2)}, u32[]{:S(2)}) collective-permute-start(f32[1,16,128]{2,1,0:T(8,128)S(1)} %get-tuple-element.18), channel_id=1, source_target_pairs={{0,8},{8,16},{16,24},{24,0},{1,9},{9,17},{17,25},{25,1},{2,10},{10... | collective-permute-start | bytes 24584 | tf_op jit(solution)/shard_map/ppermute | solution.py:582
  15.4 1.3 %copy-start.7 = (f32[16,1,16]{2,1,0:T(1,128)S(1)}, f32[16,1,16]{2,1,0:T(1,128)}, u32[]{:S(2)}) copy-start(f32[16,1,16]{2,1,0:T(1,128)} %get-tuple-element.11) | copy-start | bytes 3076
  15.4 3.4 %copy-start.6 = (f32[16,1,16]{2,1,0:T(1,128)S(1)}, f32[16,1,16]{2,1,0:T(1,128)}, u32[]{:S(2)}) copy-start(f32[16,1,16]{2,1,0:T(1,128)} %get-tuple-element.12) | copy-start | bytes 3076
  15.4 7.9 %collective-permute-start.2 = (f32[2,16,1,128]{3,2,1,0:T(1,128)S(1)}, f32[2,16,1,128]{3,2,1,0:T(1,128)S(1)}, u32[]{:S(2)}, u32[]{:S(2)}) collective-permute-start(f32[2,16,1,128]{3,2,1,0:T(1,128)S(1)} %pad_maximum_fusion), channel_id=1, source_target_pairs={{0,1},{1,0},{2,3},{3,2},{4,5},{5,4},{6,7},{7,6},{8,9},{9,8},{10,11... | collective-permute-start | bytes 49160 | tf_op jit(solution)/shard_map/ppermute | solution.py:582
  16.7 3.3 %collective-permute-start.3 = (f32[16,1,16]{2,1,0:T(1,128)S(1)}, f32[16,1,16]{2,1,0:T(1,128)S(1)}, u32[]{:S(2)}, u32[]{:S(2)}) collective-permute-start(f32[16,1,16]{2,1,0:T(1,128)S(1)} %copy-done.7), channel_id=1, source_target_pairs={{0,2},{2,4},{4,6},{6,0},{1,3},{3,5},{5,7},{7,1},{8,10},{10,12},{12... | collective-permute-start | bytes 3080 | tf_op jit(solution)/shard_map/ppermute | solution.py:582
  18.8 3.4 %collective-permute-start.4 = (f32[16,1,16]{2,1,0:T(1,128)S(1)}, f32[16,1,16]{2,1,0:T(1,128)S(1)}, u32[]{:S(2)}, u32[]{:S(2)}) collective-permute-start(f32[16,1,16]{2,1,0:T(1,128)S(1)} %copy-done.6), channel_id=1, source_target_pairs={{0,6},{2,0},{4,2},{6,4},{1,7},{3,1},{5,3},{7,5},{8,14},{10,8},{12,... | collective-permute-start | bytes 3080 | tf_op jit(solution)/shard_map/ppermute | solution.py:582
  20.0 6.6 %copy-start.4 = (f32[16,1,16]{2,1,0:T(1,128)}, f32[16,1,16]{2,1,0:T(1,128)S(1)}, u32[]{:S(2)}) copy-start(f32[16,1,16]{2,1,0:T(1,128)S(1)} %collective-permute-done.3.refs_7_) | copy-start | bytes 3076
  22.2 4.5 %copy-start.5 = (f32[16,1,16]{2,1,0:T(1,128)}, f32[16,1,16]{2,1,0:T(1,128)S(1)}, u32[]{:S(2)}) copy-start(f32[16,1,16]{2,1,0:T(1,128)S(1)} %collective-permute-done.4.refs_8_) | copy-start | bytes 3076
  22.2 4.5 %copy-start.2 = (f32[1,16,128]{2,1,0:T(8,128)}, f32[1,16,128]{2,1,0:T(8,128)S(1)}, u32[]{:S(2)}) copy-start(f32[1,16,128]{2,1,0:T(8,128)S(1)} %collective-permute-done.1.refs_5_) | copy-start | bytes 24580
  23.3 3.3 %copy-start.3 = (f32[1,16,128]{2,1,0:T(8,128)}, f32[1,16,128]{2,1,0:T(8,128)S(1)}, u32[]{:S(2)}) copy-start(f32[1,16,128]{2,1,0:T(8,128)S(1)} %collective-permute-done.refs_4_) | copy-start | bytes 24580
  23.3 3.3 %copy-start.1 = (f32[2,16,1,128]{3,2,1,0:T(1,128)}, f32[2,16,1,128]{3,2,1,0:T(1,128)S(1)}, u32[]{:S(2)}) copy-start(f32[2,16,1,128]{3,2,1,0:T(1,128)S(1)} %collective-permute-done.2.refs_6_) | copy-start | bytes 49156
  26.7 0.8 %copy-start = (f32[32,32,128]{2,1,0:T(8,128)}, f32[32,32,128]{2,1,0:T(8,128)S(1)}, u32[]{:S(2)}) copy-start(f32[32,32,128]{2,1,0:T(8,128)S(1)} %all-to-all-done.refs_2_) | copy-start | bytes 1572868
